TPU v7x, 32 devices: a whole 2x2x4 slice. The times are simulated.
32 devices in a mesh: lat: 8 (over y, x, core), lon: 4 (over z).
Axes of the slice: x: 2, y: 2, z: 4, core: 2. Of those that a mesh axis runs over, the one named last changes fastest.
Arguments:
- loadings: float32 [176, 720, 200], P('lat', 'lon'), may hold values from -60 to 60, as said below
Outputs:
- rotated: float32 [176, 720, 200], P('lat', 'lon')
- rotation: float32 [200, 200], replicated
Inputs may be any that keep to these rules, and one draw needn't show every extreme that they name: Every grid point's loadings are not all zero.
All inputs are finite; a program needn't handle non-finite values.
Results may differ from a plain program's by a relative error of at most 0.00011.
Values sent between devices are 32-bit elements; how exact they have to be, the bound alone decides.
A program may use at most 64 MiB of HBM per device.

v0:
```python
import functools
import math

import jax
import jax.numpy as jnp
import numpy as np
from jax import lax
from jax.experimental import pallas as pl
from jax.experimental.pallas import tpu as pltpu
from jax.sharding import PartitionSpec as P

SWEEPS = 2
NS_STEPS = 20
SUB = 8
LANES = 256
MESH = pl.DeviceIdType.MESH
NN = (((1,), (0,)), ((), ()))
NT = (((1,), (1,)), ((), ()))


def split(value):
    high = value.astype(jnp.bfloat16)
    low = (value - high.astype(jnp.float32)).astype(jnp.bfloat16)
    return high, low


def mm(left, right, dims=NN):
    return lax.dot_general(left, right, dims, preferred_element_type=jnp.float32)


def mm3(left, right, dims=NN):
    lh, ll = left
    rh, rl = right
    return mm(lh, rh, dims) + (mm(lh, rl, dims) + mm(ll, rh, dims))


def polar(gradient):
    squares = jnp.sum(gradient * gradient, axis=0, keepdims=True)
    norm = jnp.sqrt(jnp.sum(squares, axis=1, keepdims=True))

    def step(_, x):
        parts = split(x)
        inner = mm3(parts, parts, NT)
        return 1.5 * x - 0.5 * mm3(split(inner), parts)

    return lax.fori_loop(0, NS_STEPS, step, gradient / norm, unroll=4)


class Reduce:
    def __init__(self, me, n, n_lon, owners, bufs, sems):
        self.me, self.n, self.n_lon, self.owners = me, n, n_lon, owners
        self.src, self.got, self.full, self.rows = bufs
        self.sems = sems

    def copy(self, source, target, device, phase, sent, landed):
        return pltpu.make_async_remote_copy(
            src_ref=source,
            dst_ref=target,
            send_sem=self.sems.at[phase, sent],
            recv_sem=self.sems.at[phase + 1, landed],
            device_id=(device // self.n_lon, lax.rem(device, self.n_lon)),
            device_id_type=MESH,
        )

    def part(self, peer, source):
        return self.copy(self.src.at[peer], self.got.at[source], peer, 0, peer, source)

    def whole(self, peer, owner):
        return self.copy(self.full.at[owner], self.full.at[owner], peer, 2, peer, owner)

    def row(self, peer, source):
        return self.copy(self.rows.at[source], self.rows.at[source], peer, 4, peer, source)

    def spread(self, value):
        me, n = self.me, self.n
        self.rows[me, :, : value.shape[1]] = value
        for shift in range(1, n):
            self.row(lax.rem(me + shift, n), me).start()

    def total(self, width):
        me, n = self.me, self.n
        for shift in range(1, n):
            peer = lax.rem(me + n - shift, n)
            self.row(peer, peer).wait_recv()
        acc = self.rows[0]
        for source in range(1, n):
            acc = acc + self.rows[source]
        for shift in range(1, n):
            self.row(lax.rem(me + shift, n), me).wait_send()
        return acc[:, :width]

    def scatter(self):
        me, n = self.me, self.n
        for shift in range(1, n):
            peer = lax.rem(me + shift, n)

            @pl.when(peer < self.owners)
            def _():
                self.part(peer, me).start()

    def gather(self):
        me, n = self.me, self.n
        following = lax.rem(me + 1, n)

        @pl.when(me < self.owners)
        def _():
            acc = self.src[me]
            for shift in range(1, n):
                peer = lax.rem(me + n - shift, n)
                self.copy(self.src.at[me], self.got.at[peer], following, 0, peer, peer).wait_recv()
                acc = acc + self.got[peer]
            self.full[me] = acc
            for shift in range(1, n):
                self.whole(lax.rem(me + shift, n), me).start()

        for shift in range(1, n):
            peer = lax.rem(me + n - shift, n)

            @pl.when(peer < self.owners)
            def _():
                self.whole(following, peer).wait_recv()
                self.part(peer, me).wait_send()

        @pl.when(me < self.owners)
        def _():
            for shift in range(1, n):
                self.whole(lax.rem(me + shift, n), me).wait_send()


def kernel(n_lat, n_lon, total, weights, loadings, out, held, yh, yl, th, tl, gram, cubic,
           src1, got1, full1, rows1, src2, got2, full2, rows2, sems1, sems2, loads):
    lat_rows, lon_cols, modes = held.shape
    n = n_lat * n_lon
    owners = modes // SUB
    unroll = next(k for k in (11, 4, 3, 2, 1) if lat_rows % k == 0)
    lat, lon = lax.axis_index("lat"), lax.axis_index("lon")
    me = lat * n_lon + lon
    reduce1 = Reduce(me, n, n_lon, owners, (src1, got1, full1, rows1), sems1)
    reduce2 = Reduce(me, n, n_lon, owners, (src2, got2, full2, rows2), sems2)

    def load(j):
        return pltpu.make_async_copy(loadings.at[j], held.at[j], loads.at[j])

    for j in range(lat_rows):
        load(j).start()
    barrier = pltpu.get_barrier_semaphore()
    for shift in range(1, n):
        peer = lax.rem(me + shift, n)
        pl.semaphore_signal(barrier, inc=1, device_id=(peer // n_lon, lax.rem(peer, n_lon)),
                            device_id_type=MESH)

    def rows_of(body, init):
        def step(i, carry):
            for k in range(unroll):
                carry = body(i * unroll + k, carry)
            return carry

        return lax.fori_loop(0, lat_rows // unroll, step, init)

    def normalise(j, colsq):
        load(j).wait()
        x = held[j]
        root = weights[1, lat * lat_rows + j]
        y = x * (root / jnp.sqrt(jnp.sum(x * x, axis=1, keepdims=True) + 1e-06))
        held[j] = y
        yh[j], yl[j] = split(y)
        return colsq + jnp.sum(y * y, axis=0, keepdims=True)

    none = jnp.zeros((1, modes), jnp.float32)
    colsq = rows_of(normalise, none)
    gram[...] = jnp.zeros_like(gram)
    cubic[...] = jnp.zeros_like(cubic)
    pl.semaphore_wait(barrier, n - 1)
    reduce1.spread(colsq)

    def first(i, carry):
        grams, cubics = [], []
        for k in range(unroll):
            j = i * unroll + k
            y = held[j]
            t_parts = split(y.T)
            th[j], tl[j] = t_parts
            inverse = weights[2, lat * lat_rows + j]
            grams.append(mm3(t_parts, (yh[j], yl[j])))
            cubics.append(mm3(t_parts, split(y * y * y * inverse)))
        gram[...] += sum(grams[1:], grams[0])
        cubic[...] += sum(cubics[1:], cubics[0])
        return carry

    lax.fori_loop(0, lat_rows // unroll, first, 0)
    colsq = reduce1.total(modes)
    local = cubic[...] - gram[...] * (colsq / total)
    src1[:, :, :modes] = local.reshape(owners, SUB, modes)
    reduce1.scatter()
    cubic[...] = jnp.zeros_like(cubic)
    reduce1.gather()
    rotation = polar(full1[:, :, :modes].reshape(modes, modes))
    r_parts = split(rotation)

    def spin(j, colsq):
        spun = mm3((yh[j], yl[j]), r_parts)
        held[j] = spun
        return colsq + jnp.sum(spun * spun, axis=0, keepdims=True)

    reduce2.spread(rows_of(spin, none))

    def second(i, carry):
        cubics = []
        for k in range(unroll):
            j = i * unroll + k
            spun = held[j]
            inverse = weights[2, lat * lat_rows + j]
            cubics.append(mm3((th[j], tl[j]), split(spun * spun * spun * inverse)))
        cubic[...] += sum(cubics[1:], cubics[0])
        return carry

    lax.fori_loop(0, lat_rows // unroll, second, 0)
    turned = mm3(split(gram[...]), r_parts)
    colsq = reduce2.total(modes)
    local = cubic[...] - turned * (colsq / total)
    src2[:, :, :modes] = local.reshape(owners, SUB, modes)
    reduce2.scatter()
    reduce2.gather()
    out[...] = polar(full2[:, :, :modes].reshape(modes, modes))


def latitude_weight(lat_total):
    rows = np.arange(lat_total, dtype=np.float32)
    degrees = np.float32(-90.0) + (rows + np.float32(0.5)) * np.float32(180.0 / lat_total)
    return np.cos(degrees * np.float32(math.pi / 180.0)).astype(np.float32)


def shards(n_lat, n_lon, loadings):
    lat_rows, lon_cols, modes = loadings.shape
    n = n_lat * n_lon
    owners = modes // SUB
    assert modes % SUB == 0 and owners <= n and modes <= LANES
    weights = latitude_weight(lat_rows * n_lat)
    total = float(np.sum(weights, dtype=np.float32) * np.float32(lon_cols * n_lon))
    table = jnp.asarray(np.stack([weights, np.sqrt(weights), 1.0 / weights]).astype(np.float32))
    f32, bf16 = jnp.float32, jnp.bfloat16

    bufs = [
        pltpu.VMEM((owners, SUB, LANES), f32),
        pltpu.VMEM((n, SUB, LANES), f32),
        pltpu.VMEM((owners, SUB, LANES), f32),
        pltpu.VMEM((n, 1, LANES), f32),
    ]

    rotation = pl.pallas_call(
        functools.partial(kernel, n_lat, n_lon, total),
        out_shape=jax.ShapeDtypeStruct((modes, modes), f32),
        in_specs=[
            pl.BlockSpec(memory_space=pltpu.SMEM),
            pl.BlockSpec(memory_space=pl.ANY),
        ],
        out_specs=pl.BlockSpec(memory_space=pltpu.VMEM),
        scratch_shapes=[
            pltpu.VMEM((lat_rows, lon_cols, modes), f32),
            pltpu.VMEM((lat_rows, lon_cols, modes), bf16),
            pltpu.VMEM((lat_rows, lon_cols, modes), bf16),
            pltpu.VMEM((lat_rows, modes, lon_cols), bf16),
            pltpu.VMEM((lat_rows, modes, lon_cols), bf16),
            pltpu.VMEM((modes, modes), f32),
            pltpu.VMEM((modes, modes), f32),
            *bufs,
            *bufs,
            pltpu.SemaphoreType.DMA((6, n)),
            pltpu.SemaphoreType.DMA((6, n)),
            pltpu.SemaphoreType.DMA((lat_rows,)),
        ],
        compiler_params=pltpu.CompilerParams(
            collective_id=0, has_side_effects=True, vmem_limit_bytes=60 * 1024 * 1024
        ),
    )(table, loadings)
    rotated = jnp.einsum("abk,kl->abl", loadings, rotation, precision=lax.Precision.HIGH)
    return (rotated, rotation)


def solution(mesh):
    return jax.shard_map(
        functools.partial(shards, mesh.shape["lat"], mesh.shape["lon"]),
        mesh=mesh,
        in_specs=(P("lat", "lon", None),),
        out_specs=(P("lat", "lon", None), P()),
        check_vma=False,
    )
```

profile of v0, /device:TPU:0, one launch (start us, length us, event | category | flops | bytes accessed | tf_op | source)
XLA Modules:
  0.0 83.2 jit_solution(3398472903786699602)
XLA Ops:
  0.6 75.7 %shard_map.41 = f32[200,200]{1,0:T(8,128)} custom-call(f32[3,176]{1,0:T(4,128)} %constant.2.clone.weights, f32[22,180,200]{2,1,0:T(8,128)} %loadings.1), custom_call_target="tpu_custom_call" | custom-call | tf_op jit(solution)/shard_map/pallas_call | solution.py:250
  76.4 0.0 copy-start
  76.4 6.1 %convolution_bitcast_fusion = f32[22,180,200]{2,1,0:T(8,128)} fusion(f32[22,180,200]{2,1,0:T(8,128)} %loadings.1, f32[200,200]{1,0:T(8,128)} %shard_map.41), kind=kOutput, calls=%fused_computation | convolution fusion | flops 950400000 | bytes 6496000 | tf_op jit(solution)/shard_map/abk,kl->abl/dot_general | solution.py:276
  82.5 0.0 copy-done
  82.5 0.7 copy.5
Async XLA Ops:
  76.4 6.2 %copy-start = (f32[200,200]{1,0:T(8,128)S(1)}, f32[200,200]{1,0:T(8,128)}, u32[]{:S(2)}) copy-start(f32[200,200]{1,0:T(8,128)} %shard_map.41) | copy-start | bytes 480004
where the time goes:
time: 83.4 us; the launch traced here: 83.2 us
  Pallas kernels  75.7 us (91%)
  matrix products  6.14 us (7%)
    pallas_call x1, Pallas kernels, shards(): pl.pallas_call(functools.partial(kernel, n_lat, n_lon, total), out_shape=...  75.7 us
    dot_general x1, matrix products, shards(): jnp.einsum('abk,kl->abl', loadings, rotation, precision=lax.Precision.HIGH)  6.14 us

commit v1 on v0

v1 whole, which is shorter than its diff:
```python
import functools
import math

import jax
import jax.numpy as jnp
import numpy as np
from jax import lax
from jax.experimental import pallas as pl
from jax.experimental.pallas import tpu as pltpu
from jax.sharding import PartitionSpec as P

SWEEPS = 2
NS_STEPS = 20
SUB = 8
LANES = 256
CORES = 2
MESH = pl.DeviceIdType.MESH
NN = (((1,), (0,)), ((), ()))
NT = (((1,), (1,)), ((), ()))


def split(value):
    high = value.astype(jnp.bfloat16)
    low = (value - high.astype(jnp.float32)).astype(jnp.bfloat16)
    return high, low


def mm(left, right, dims=NN):
    return lax.dot_general(left, right, dims, preferred_element_type=jnp.float32)


def mm3(left, right, dims=NN):
    lh, ll = left
    rh, rl = right
    return mm(lh, rh, dims) + (mm(lh, rl, dims) + mm(ll, rh, dims))


def polar(gradient):
    squares = jnp.sum(gradient * gradient, axis=0, keepdims=True)
    norm = jnp.sqrt(jnp.sum(squares, axis=1, keepdims=True))

    def step(_, x):
        parts = split(x)
        inner = mm3(parts, parts, NT)
        return 1.5 * x - 0.5 * mm3(split(inner), parts)

    return lax.fori_loop(0, NS_STEPS, step, gradient / norm, unroll=4)


class Mesh:
    def __init__(self, n_lat, n_lon):
        self.n_lon, self.n = n_lon, n_lat * n_lon
        self.chips = self.n // CORES
        lat, lon = lax.axis_index("lat"), lax.axis_index("lon")
        self.lat = lat
        self.me = lat * n_lon + lon
        self.core = lax.rem(lat, CORES)
        self.other = 1 - self.core
        self.chip = (lat // CORES) * n_lon + lon

    def device(self, index):
        return index // self.n_lon, lax.rem(index, self.n_lon)

    def seat(self, chip, core):
        return (chip // self.n_lon) * CORES + core, lax.rem(chip, self.n_lon)


def remote(source, target, sems, phase, device):
    return pltpu.make_async_remote_copy(
        src_ref=source,
        dst_ref=target,
        send_sem=sems.at[phase, 0],
        recv_sem=sems.at[phase, 1],
        device_id=device,
        device_id_type=MESH,
    )


class Reduce:
    def __init__(self, mesh, owners, bufs, sems):
        self.mesh, self.owners = mesh, owners
        self.part, self.peer, self.chip_sum, self.got, self.full, self.rows = bufs
        self.sems = sems

    def spread(self, value):
        mesh = self.mesh
        self.rows[mesh.me, :, : value.shape[1]] = value
        for shift in range(1, mesh.n):
            row = self.rows.at[mesh.me]
            remote(row, row, self.sems, 0, mesh.device(lax.rem(mesh.me + shift, mesh.n))).start()

    def others(self):
        rest = self.rows.at[pl.ds(0, self.mesh.n - 1)]
        return remote(rest, rest, self.sems, 0, self.mesh.device(self.mesh.me))

    def total(self, width):
        self.others().wait_recv()
        acc = self.rows[0]
        for source in range(1, self.mesh.n):
            acc = acc + self.rows[source]
        return acc[:, :width]

    def swap(self):
        mesh = self.mesh
        return remote(self.part.at[mesh.other], self.peer, self.sems, 1,
                      mesh.seat(mesh.chip, mesh.other))

    def scatter(self, owner):
        mesh = self.mesh
        return remote(self.chip_sum.at[owner], self.got.at[mesh.chip], self.sems, 2,
                      mesh.seat(owner, mesh.core))

    def gather(self, chip, blocks):
        mesh = self.mesh
        block = self.full.at[mesh.core, blocks]
        return remote(block, block, self.sems, 3, mesh.seat(chip, mesh.core))

    def share(self):
        mesh = self.mesh
        half = self.full.at[mesh.core]
        return remote(half, half, self.sems, 4, mesh.seat(mesh.chip, mesh.other))

    def reduce(self):
        mesh, owners = self.mesh, self.owners
        chip, chips = mesh.chip, mesh.chips
        self.swap().start()
        self.swap().wait_recv()
        self.chip_sum[...] = self.part[mesh.core] + self.peer[...]
        for shift in range(1, chips):
            owner = lax.rem(chip + shift, chips)

            @pl.when(owner < owners)
            def _():
                self.scatter(owner).start()

        @pl.when(chip < owners)
        def _():
            rest = self.got.at[pl.ds(0, chips - 1)]
            remote(rest, rest, self.sems, 2, mesh.seat(chip, mesh.core)).wait_recv()
            acc = self.chip_sum[chip]
            for shift in range(1, chips):
                acc = acc + self.got[lax.rem(chip + shift, chips)]
            self.full[mesh.core, chip] = acc
            for shift in range(1, chips):
                self.gather(lax.rem(chip + shift, chips), chip).start()
            self.gather(chip, pl.ds(0, owners - 1)).wait_recv()

        @pl.when(chip >= owners)
        def _():
            self.gather(chip, pl.ds(0, owners)).wait_recv()

        self.share().start()
        self.share().wait_recv()

    def finish(self):
        mesh, owners = self.mesh, self.owners
        chip, chips = mesh.chip, mesh.chips
        self.others().wait_send()
        self.swap().wait_send()
        self.share().wait_send()

        @pl.when(chip < owners)
        def _():
            rest = self.got.at[pl.ds(0, owners - 1)]
            remote(rest, rest, self.sems, 2, mesh.seat(chip, mesh.core)).wait_send()
            rest = self.got.at[pl.ds(0, chips - 1)]
            remote(rest, rest, self.sems, 3, mesh.seat(chip, mesh.core)).wait_send()

        @pl.when(chip >= owners)
        def _():
            rest = self.got.at[pl.ds(0, owners)]
            remote(rest, rest, self.sems, 2, mesh.seat(chip, mesh.core)).wait_send()


def halves(value, owners):
    modes = value.shape[0]
    rows = owners * SUB
    return value[:rows].reshape(owners, SUB, modes), value[rows:].reshape(-1, SUB, modes)


def store_halves(part, value, owners):
    modes = value.shape[1]
    low, high = halves(value, owners)
    part[0, :, :, :modes] = low
    part[1, : high.shape[0], :, :modes] = high


def whole(full, modes):
    blocks = [full[0, :, :, :modes].reshape(-1, modes), full[1, :, :, :modes].reshape(-1, modes)]
    return jnp.concatenate(blocks, axis=0)[:modes]


def kernel(n_lat, n_lon, total, weights, loadings, out, held, yh, yl, th, tl, gram, cubic,
           part1, peer1, sum1, got1, full1, rows1, part2, peer2, sum2, got2, full2, rows2,
           sems1, sems2, loads):
    lat_rows, lon_cols, modes = held.shape
    mesh = Mesh(n_lat, n_lon)
    n, me, lat = mesh.n, mesh.me, mesh.lat
    owners = part1.shape[1]
    unroll = next(k for k in (11, 4, 3, 2, 1) if lat_rows % k == 0)
    reduce1 = Reduce(mesh, owners, (part1, peer1, sum1, got1, full1, rows1), sems1)
    reduce2 = Reduce(mesh, owners, (part2, peer2, sum2, got2, full2, rows2), sems2)

    def load(j):
        return pltpu.make_async_copy(loadings.at[j], held.at[j], loads.at[j])

    for j in range(lat_rows):
        load(j).start()
    barrier = pltpu.get_barrier_semaphore()
    for shift in range(1, n):
        peer = lax.rem(me + shift, n)
        pl.semaphore_signal(barrier, inc=1, device_id=mesh.device(peer), device_id_type=MESH)

    def rows_of(body, init):
        def step(i, carry):
            for k in range(unroll):
                carry = body(i * unroll + k, carry)
            return carry

        return lax.fori_loop(0, lat_rows // unroll, step, init)

    def normalise(j, colsq):
        load(j).wait()
        x = held[j]
        root = weights[1, lat * lat_rows + j]
        y = x * (root / jnp.sqrt(jnp.sum(x * x, axis=1, keepdims=True) + 1e-06))
        held[j] = y
        yh[j], yl[j] = split(y)
        return colsq + jnp.sum(y * y, axis=0, keepdims=True)

    none = jnp.zeros((1, modes), jnp.float32)
    colsq = rows_of(normalise, none)
    gram[...] = jnp.zeros_like(gram)
    cubic[...] = jnp.zeros_like(cubic)
    part1[...] = jnp.zeros_like(part1)
    part2[...] = jnp.zeros_like(part2)
    pl.semaphore_wait(barrier, n - 1)
    reduce1.spread(colsq)

    def first(i, carry):
        grams, cubics = [], []
        for k in range(unroll):
            j = i * unroll + k
            y = held[j]
            t_parts = split(y.T)
            th[j], tl[j] = t_parts
            inverse = weights[2, lat * lat_rows + j]
            grams.append(mm3(t_parts, (yh[j], yl[j])))
            cubics.append(mm3(t_parts, split(y * y * y * inverse)))
        gram[...] += sum(grams[1:], grams[0])
        cubic[...] += sum(cubics[1:], cubics[0])
        return carry

    lax.fori_loop(0, lat_rows // unroll, first, 0)
    colsq = reduce1.total(modes)
    store_halves(part1, cubic[...] - gram[...] * (colsq / total), owners)
    reduce1.reduce()
    cubic[...] = jnp.zeros_like(cubic)
    rotation = polar(whole(full1, modes))
    r_parts = split(rotation)

    def spin(j, colsq):
        spun = mm3((yh[j], yl[j]), r_parts)
        held[j] = spun
        return colsq + jnp.sum(spun * spun, axis=0, keepdims=True)

    reduce2.spread(rows_of(spin, none))

    def second(i, carry):
        cubics = []
        for k in range(unroll):
            j = i * unroll + k
            spun = held[j]
            inverse = weights[2, lat * lat_rows + j]
            cubics.append(mm3((th[j], tl[j]), split(spun * spun * spun * inverse)))
        cubic[...] += sum(cubics[1:], cubics[0])
        return carry

    lax.fori_loop(0, lat_rows // unroll, second, 0)
    turned = mm3(split(gram[...]), r_parts)
    colsq = reduce2.total(modes)
    store_halves(part2, cubic[...] - turned * (colsq / total), owners)
    reduce2.reduce()
    out[...] = whole(full2, modes)
    reduce1.finish()
    reduce2.finish()


def turn(gradient, loadings, rotated, rotation, held, result, load, stores):
    lat_rows = held.shape[0]
    fetch = pltpu.make_async_copy(loadings, held, load)
    fetch.start()
    result[...] = polar(gradient[...])
    save = pltpu.make_async_copy(result, rotation, stores.at[0])
    save.start()
    r_parts = split(result[...])
    fetch.wait()
    unroll = next(k for k in (2, 1) if lat_rows % k == 0)

    def step(i, carry):
        for k in range(unroll):
            j = i * unroll + k
            held[j] = mm3(split(held[j]), r_parts)
            pltpu.make_async_copy(held.at[j], rotated.at[j], stores.at[1]).start()
        return carry

    lax.fori_loop(0, lat_rows // unroll, step, 0)
    save.wait()
    pltpu.make_async_copy(held, rotated, stores.at[1]).wait()


def latitude_weight(lat_total):
    rows = np.arange(lat_total, dtype=np.float32)
    degrees = np.float32(-90.0) + (rows + np.float32(0.5)) * np.float32(180.0 / lat_total)
    return np.cos(degrees * np.float32(math.pi / 180.0)).astype(np.float32)


def shards(n_lat, n_lon, loadings):
    lat_rows, lon_cols, modes = loadings.shape
    n = n_lat * n_lon
    owners = -(-modes // (CORES * SUB))
    assert n_lat % CORES == 0 and modes % SUB == 0 and modes <= LANES
    assert 1 < owners <= n // CORES
    weights = latitude_weight(lat_rows * n_lat)
    total = float(np.sum(weights, dtype=np.float32) * np.float32(lon_cols * n_lon))
    table = jnp.asarray(np.stack([weights, np.sqrt(weights), 1.0 / weights]).astype(np.float32))
    f32, bf16 = jnp.float32, jnp.bfloat16

    bufs = [
        pltpu.VMEM((CORES, owners, SUB, LANES), f32),
        pltpu.VMEM((owners, SUB, LANES), f32),
        pltpu.VMEM((owners, SUB, LANES), f32),
        pltpu.VMEM((n // CORES, SUB, LANES), f32),
        pltpu.VMEM((CORES, owners, SUB, LANES), f32),
        pltpu.VMEM((n, 1, LANES), f32),
    ]

    gradient = pl.pallas_call(
        functools.partial(kernel, n_lat, n_lon, total),
        out_shape=jax.ShapeDtypeStruct((modes, modes), f32),
        in_specs=[
            pl.BlockSpec(memory_space=pltpu.SMEM),
            pl.BlockSpec(memory_space=pl.ANY),
        ],
        out_specs=pl.BlockSpec(memory_space=pltpu.VMEM),
        scratch_shapes=[
            pltpu.VMEM((lat_rows, lon_cols, modes), f32),
            pltpu.VMEM((lat_rows, lon_cols, modes), bf16),
            pltpu.VMEM((lat_rows, lon_cols, modes), bf16),
            pltpu.VMEM((lat_rows, modes, lon_cols), bf16),
            pltpu.VMEM((lat_rows, modes, lon_cols), bf16),
            pltpu.VMEM((modes, modes), f32),
            pltpu.VMEM((modes, modes), f32),
            *bufs,
            *bufs,
            pltpu.SemaphoreType.DMA((5, 2)),
            pltpu.SemaphoreType.DMA((5, 2)),
            pltpu.SemaphoreType.DMA((lat_rows,)),
        ],
        compiler_params=pltpu.CompilerParams(
            collective_id=0, has_side_effects=True, vmem_limit_bytes=60 * 1024 * 1024
        ),
    )(table, loadings)
    return pl.pallas_call(
        turn,
        out_shape=(
            jax.ShapeDtypeStruct(loadings.shape, f32),
            jax.ShapeDtypeStruct((modes, modes), f32),
        ),
        in_specs=[
            pl.BlockSpec(memory_space=pltpu.VMEM),
            pl.BlockSpec(memory_space=pl.ANY),
        ],
        out_specs=(
            pl.BlockSpec(memory_space=pl.ANY),
            pl.BlockSpec(memory_space=pl.ANY),
        ),
        scratch_shapes=[
            pltpu.VMEM((lat_rows, lon_cols, modes), f32),
            pltpu.VMEM((modes, modes), f32),
            pltpu.SemaphoreType.DMA,
            pltpu.SemaphoreType.DMA((2,)),
        ],
        compiler_params=pltpu.CompilerParams(vmem_limit_bytes=60 * 1024 * 1024),
    )(gradient, loadings)


def solution(mesh):
    return jax.shard_map(
        functools.partial(shards, mesh.shape["lat"], mesh.shape["lon"]),
        mesh=mesh,
        in_specs=(P("lat", "lon", None),),
        out_specs=(P("lat", "lon", None), P()),
        check_vma=False,
    )
```

time: 83.4 us -> 73.7 us (0.88)
  matrix products: 6.14 us -> 0 us
  Pallas kernels: 75.7 us -> 72.9 us
    pallas_call x1, Pallas kernels: 75.7 us -> 56.8 us  [shards(): pl.pallas_call(functools.partial(kernel, n_lat, n_lon, total), out_shape=...]
    pallas_call x0 -> x1, Pallas kernels: none -> 16.1 us  [shards(): pl.pallas_call(turn, out_shape=(jax.ShapeDtypeStruct(loadings.shape, f32)...]
    dot_general x1 -> x0, matrix products: 6.14 us -> none  [shards(): jnp.einsum('abk,kl->abl', loadings, rotation, precision=lax.Precision.HIGH)]
where the time goes in v1:
time: 73.7 us; the launch traced here: 73.5 us
  Pallas kernels  72.9 us (99%)
    pallas_call x1, Pallas kernels, shards(): pl.pallas_call(functools.partial(kernel, n_lat, n_lon, total), out_shape=...  56.8 us
    pallas_call x1, Pallas kernels, shards(): pl.pallas_call(turn, out_shape=(jax.ShapeDtypeStruct(loadings.shape, f32)...  16.1 us

profile of v1, /device:TPU:0, one launch (start us, length us, event | category | flops | bytes accessed | tf_op | source)
XLA Modules:
  0.0 73.5 jit_solution(11037892923464978791)
XLA Ops:
  0.6 56.8 %shard_map.41.gradient = f32[200,200]{1,0:T(8,128)} custom-call(f32[3,176]{1,0:T(4,128)} %constant.2.clone.weights, f32[22,180,200]{2,1,0:T(8,128)} %loadings.3), custom_call_target="tpu_custom_call" | custom-call | tf_op jit(solution)/shard_map/pallas_call | solution.py:338
  57.4 16.1 %shard_map.42 = (f32[22,180,200]{2,1,0:T(8,128)}, f32[200,200]{1,0:T(8,128)}) custom-call(f32[200,200]{1,0:T(8,128)} %shard_map.41.gradient, f32[22,180,200]{2,1,0:T(8,128)} %loadings.3), custom_call_target="tpu_custom_call" | custom-call | tf_op jit(solution)/shard_map/pallas_call | solution.py:364

commit v2 on v1

--- a/solution.py
+++ b/solution.py
@@ -14,6 +14,7 @@
 SUB = 8
 LANES = 256
 CORES = 2
+DEPTH = 256
 MESH = pl.DeviceIdType.MESH
 NN = (((1,), (0,)), ((), ()))
 NT = (((1,), (1,)), ((), ()))
@@ -35,16 +36,29 @@
     return mm(lh, rh, dims) + (mm(lh, rl, dims) + mm(ll, rh, dims))
 
 
+def mm_rows(rows, right, dims):
+    high, low = rows
+    count = high.shape[0]
+    both = mm(jnp.concatenate([high, low], axis=0), right[0], dims)
+    return both[:count] + (both[count:] + mm(high, right[1], dims))
+
+
 def polar(gradient):
     squares = jnp.sum(gradient * gradient, axis=0, keepdims=True)
     norm = jnp.sqrt(jnp.sum(squares, axis=1, keepdims=True))
-
-    def step(_, x):
-        parts = split(x)
-        inner = mm3(parts, parts, NT)
-        return 1.5 * x - 0.5 * mm3(split(inner), parts)
-
-    return lax.fori_loop(0, NS_STEPS, step, gradient / norm, unroll=4)
+    modes = gradient.shape[0]
+    cut = -(-modes // (4 * SUB)) * 2 * SUB
+
+    def step(_, rows):
+        pieces = [split(x) for x in rows]
+        parts = [jnp.concatenate(side, axis=0) for side in zip(*pieces)]
+        inner = [mm_rows(piece, parts, NT) for piece in pieces]
+        turned = [mm_rows(split(x), parts, NN) for x in inner]
+        return tuple(1.5 * x - 0.5 * y for x, y in zip(rows, turned))
+
+    start = gradient / norm
+    rows = lax.fori_loop(0, NS_STEPS, step, (start[:cut], start[cut:]), unroll=4)
+    return jnp.concatenate(rows, axis=0)
 
 
 class Mesh:
@@ -77,9 +91,10 @@
 
 
 class Reduce:
-    def __init__(self, mesh, owners, bufs, sems):
+    def __init__(self, mesh, owners, modes, bufs, sems):
         self.mesh, self.owners = mesh, owners
         self.part, self.peer, self.chip_sum, self.got, self.full, self.rows = bufs
+        self.modes = modes
         self.sems = sems
 
     def spread(self, value):
@@ -93,17 +108,29 @@
         rest = self.rows.at[pl.ds(0, self.mesh.n - 1)]
         return remote(rest, rest, self.sems, 0, self.mesh.device(self.mesh.me))
 
-    def total(self, width):
+    def total(self):
         self.others().wait_recv()
         acc = self.rows[0]
         for source in range(1, self.mesh.n):
             acc = acc + self.rows[source]
-        return acc[:, :width]
-
-    def swap(self):
+        return acc
+
+    def swap(self, term):
         mesh = self.mesh
-        return remote(self.part.at[mesh.other], self.peer, self.sems, 1,
+        return remote(self.part.at[term, mesh.other], self.peer.at[term], self.sems, 4 + term,
                       mesh.seat(mesh.chip, mesh.other))
+
+    def send(self, term, value):
+        rows = self.owners * SUB
+        modes = self.modes
+        low, high = value[:rows], value[rows:]
+        self.part[term, 0, :, :, :modes] = low.reshape(-1, SUB, modes)
+        self.part[term, 1, : high.shape[0] // SUB, :, :modes] = high.reshape(-1, SUB, modes)
+        self.swap(term).start()
+
+    def joined(self, term):
+        self.swap(term).wait_recv()
+        return self.part[term, self.mesh.core] + self.peer[term]
 
     def scatter(self, owner):
         mesh = self.mesh
@@ -118,14 +145,12 @@
     def share(self):
         mesh = self.mesh
         half = self.full.at[mesh.core]
-        return remote(half, half, self.sems, 4, mesh.seat(mesh.chip, mesh.other))
-
-    def reduce(self):
+        return remote(half, half, self.sems, 1, mesh.seat(mesh.chip, mesh.other))
+
+    def reduce(self, value):
         mesh, owners = self.mesh, self.owners
         chip, chips = mesh.chip, mesh.chips
-        self.swap().start()
-        self.swap().wait_recv()
-        self.chip_sum[...] = self.part[mesh.core] + self.peer[...]
+        self.chip_sum[...] = value
         for shift in range(1, chips):
             owner = lax.rem(chip + shift, chips)
 
@@ -156,7 +181,8 @@
         mesh, owners = self.mesh, self.owners
         chip, chips = mesh.chip, mesh.chips
         self.others().wait_send()
-        self.swap().wait_send()
+        for term in range(2):
+            self.swap(term).wait_send()
         self.share().wait_send()
 
         @pl.when(chip < owners)
@@ -172,17 +198,9 @@
             remote(rest, rest, self.sems, 2, mesh.seat(chip, mesh.core)).wait_send()
 
 
-def halves(value, owners):
-    modes = value.shape[0]
-    rows = owners * SUB
-    return value[:rows].reshape(owners, SUB, modes), value[rows:].reshape(-1, SUB, modes)
-
-
-def store_halves(part, value, owners):
-    modes = value.shape[1]
-    low, high = halves(value, owners)
-    part[0, :, :, :modes] = low
-    part[1, : high.shape[0], :, :modes] = high
+def loads_group(lat_rows, lon_cols):
+    return next(k for k in range(1, lat_rows + 1)
+                if lat_rows % k == 0 and k * lon_cols % SUB == 0)
 
 
 def whole(full, modes):
@@ -190,97 +208,115 @@
     return jnp.concatenate(blocks, axis=0)[:modes]
 
 
-def kernel(n_lat, n_lon, total, weights, loadings, out, held, yh, yl, th, tl, gram, cubic,
-           part1, peer1, sum1, got1, full1, rows1, part2, peer2, sum2, got2, full2, rows2,
-           sems1, sems2, loads):
+def kernel(n_lat, n_lon, total, weights, loadings, out, held, flat, scale, yh, yl, th, tl, ch, cl,
+           half_gram, cubic, part1, peer1, sum1, got1, full1, rows1,
+           part2, peer2, sum2, got2, full2, rows2, sems1, sems2, loads):
     lat_rows, lon_cols, modes = held.shape
+    chunks, depth, _ = yh.shape
+    points = lat_rows * lon_cols
+    group = loads_group(lat_rows, lon_cols)
     mesh = Mesh(n_lat, n_lon)
     n, me, lat = mesh.n, mesh.me, mesh.lat
-    owners = part1.shape[1]
-    unroll = next(k for k in (11, 4, 3, 2, 1) if lat_rows % k == 0)
-    reduce1 = Reduce(mesh, owners, (part1, peer1, sum1, got1, full1, rows1), sems1)
-    reduce2 = Reduce(mesh, owners, (part2, peer2, sum2, got2, full2, rows2), sems2)
-
-    def load(j):
-        return pltpu.make_async_copy(loadings.at[j], held.at[j], loads.at[j])
-
-    for j in range(lat_rows):
-        load(j).start()
+    owners = sum1.shape[0]
+    reduce1 = Reduce(mesh, owners, modes, (part1, peer1, sum1, got1, full1, rows1), sems1)
+    reduce2 = Reduce(mesh, owners, modes, (part2, peer2, sum2, got2, full2, rows2), sems2)
+
+    def load(i):
+        rows = pl.ds(i * group, group)
+        return pltpu.make_async_copy(loadings.at[rows], held.at[rows], loads.at[i])
+
+    for i in range(lat_rows // group):
+        load(i).start()
     barrier = pltpu.get_barrier_semaphore()
     for shift in range(1, n):
         peer = lax.rem(me + shift, n)
         pl.semaphore_signal(barrier, inc=1, device_id=mesh.device(peer), device_id_type=MESH)
 
-    def rows_of(body, init):
-        def step(i, carry):
-            for k in range(unroll):
-                carry = body(i * unroll + k, carry)
-            return carry
-
-        return lax.fori_loop(0, lat_rows // unroll, step, init)
-
-    def normalise(j, colsq):
-        load(j).wait()
-        x = held[j]
-        root = weights[1, lat * lat_rows + j]
-        y = x * (root / jnp.sqrt(jnp.sum(x * x, axis=1, keepdims=True) + 1e-06))
-        held[j] = y
-        yh[j], yl[j] = split(y)
-        return colsq + jnp.sum(y * y, axis=0, keepdims=True)
+    flat[points:, :] = jnp.zeros((chunks * depth - points, modes), jnp.float32)
+    scale[points:, :] = jnp.zeros((chunks * depth - points, scale.shape[1]), jnp.float32)
+    half_gram[...] = jnp.zeros_like(half_gram)
+    cubic[...] = jnp.zeros_like(cubic)
+
+    def normalise(i, colsq):
+        load(i).wait()
+        ys, scales = [], []
+        for k in range(group):
+            j = i * group + k
+            x = held[j]
+            root = weights[1, lat * lat_rows + j]
+            inverse = weights[2, lat * lat_rows + j]
+            y = x * (root * lax.rsqrt(jnp.sum(x * x, axis=1, keepdims=True) + 1e-06))
+            ys.append(y)
+            scales.append(jnp.full((lon_cols, scale.shape[1]), inverse, jnp.float32))
+            colsq = colsq + jnp.sum(y * y, axis=0, keepdims=True)
+        rows = pl.ds(pl.multiple_of(i * group * lon_cols, SUB), group * lon_cols)
+        flat[rows, :] = jnp.concatenate(ys, axis=0)
+        scale[rows, :] = jnp.concatenate(scales, axis=0)
+        return colsq
 
     none = jnp.zeros((1, modes), jnp.float32)
-    colsq = rows_of(normalise, none)
-    gram[...] = jnp.zeros_like(gram)
-    cubic[...] = jnp.zeros_like(cubic)
-    part1[...] = jnp.zeros_like(part1)
-    part2[...] = jnp.zeros_like(part2)
+    colsq = lax.fori_loop(0, lat_rows // group, normalise, none)
     pl.semaphore_wait(barrier, n - 1)
     reduce1.spread(colsq)
+
+    def cubed(value, c):
+        rows = pl.ds(pl.multiple_of(c * depth, depth), depth)
+        factor = scale[rows, :]
+        factor = jnp.concatenate([factor] * (LANES // factor.shape[1]), axis=1)[:, :modes]
+        return split(value * value * value * factor)
+
+    unroll = next(k for k in (4, 3, 2, 1) if chunks % k == 0)
 
     def first(i, carry):
         grams, cubics = [], []
         for k in range(unroll):
-            j = i * unroll + k
-            y = held[j]
+            c = i * unroll + k
+            y = flat[pl.ds(pl.multiple_of(c * depth, depth), depth), :]
+            high, low = split(y)
+            yh[c], yl[c] = high, low
             t_parts = split(y.T)
-            th[j], tl[j] = t_parts
-            inverse = weights[2, lat * lat_rows + j]
-            grams.append(mm3(t_parts, (yh[j], yl[j])))
-            cubics.append(mm3(t_parts, split(y * y * y * inverse)))
-        gram[...] += sum(grams[1:], grams[0])
+            th[c], tl[c] = t_parts
+            grams.append(mm(t_parts[0], 0.5 * high) + mm(t_parts[0], low))
+            cubics.append(mm3(t_parts, cubed(y, c)))
+        half_gram[...] += sum(grams[1:], grams[0])
         cubic[...] += sum(cubics[1:], cubics[0])
         return carry
 
-    lax.fori_loop(0, lat_rows // unroll, first, 0)
-    colsq = reduce1.total(modes)
-    store_halves(part1, cubic[...] - gram[...] * (colsq / total), owners)
-    reduce1.reduce()
+    lax.fori_loop(0, chunks // unroll, first, 0)
+    reduce1.send(0, cubic[...])
+    half = half_gram[...]
+    gram = half + half.T
+    half_gram[...] = gram
+    reduce1.send(1, gram)
     cubic[...] = jnp.zeros_like(cubic)
+    joined = [reduce1.joined(term) for term in range(2)]
+    reduce1.reduce(joined[0] - joined[1] * (reduce1.total() / total))
     rotation = polar(whole(full1, modes))
     r_parts = split(rotation)
 
-    def spin(j, colsq):
-        spun = mm3((yh[j], yl[j]), r_parts)
-        held[j] = spun
-        return colsq + jnp.sum(spun * spun, axis=0, keepdims=True)
-
-    reduce2.spread(rows_of(spin, none))
+    turned = mm3(split(half_gram[...]), r_parts)
+    reduce2.spread(jnp.sum(turned * rotation, axis=0, keepdims=True))
+    reduce2.send(1, turned)
+
+    def spin(i, carry):
+        for k in range(8):
+            c = i * 8 + k
+            ch[c], cl[c] = cubed(mm3((yh[c], yl[c]), r_parts), c)
+        return carry
 
     def second(i, carry):
         cubics = []
-        for k in range(unroll):
-            j = i * unroll + k
-            spun = held[j]
-            inverse = weights[2, lat * lat_rows + j]
-            cubics.append(mm3((th[j], tl[j]), split(spun * spun * spun * inverse)))
+        for k in range(8):
+            c = i * 8 + k
+            cubics.append(mm3((th[c], tl[c]), (ch[c], cl[c])))
         cubic[...] += sum(cubics[1:], cubics[0])
         return carry
 
-    lax.fori_loop(0, lat_rows // unroll, second, 0)
-    turned = mm3(split(gram[...]), r_parts)
-    colsq = reduce2.total(modes)
-    store_halves(part2, cubic[...] - turned * (colsq / total), owners)
-    reduce2.reduce()
+    lax.fori_loop(0, chunks // 8, spin, 0)
+    lax.fori_loop(0, chunks // 8, second, 0)
+    reduce2.send(0, cubic[...])
+    joined = [reduce2.joined(term) for term in range(2)]
+    reduce2.reduce(joined[0] - joined[1] * (reduce2.total() / total))
     out[...] = whole(full2, modes)
     reduce1.finish()
     reduce2.finish()
@@ -295,7 +331,7 @@
     save.start()
     r_parts = split(result[...])
     fetch.wait()
-    unroll = next(k for k in (2, 1) if lat_rows % k == 0)
+    unroll = next(k for k in (11, 4, 3, 2, 1) if lat_rows % k == 0)
 
     def step(i, carry):
         for k in range(unroll):
@@ -327,13 +363,16 @@
     f32, bf16 = jnp.float32, jnp.bfloat16
 
     bufs = [
-        pltpu.VMEM((CORES, owners, SUB, LANES), f32),
-        pltpu.VMEM((owners, SUB, LANES), f32),
+        pltpu.VMEM((2, CORES, owners, SUB, LANES), f32),
+        pltpu.VMEM((2, owners, SUB, LANES), f32),
         pltpu.VMEM((owners, SUB, LANES), f32),
         pltpu.VMEM((n // CORES, SUB, LANES), f32),
         pltpu.VMEM((CORES, owners, SUB, LANES), f32),
         pltpu.VMEM((n, 1, LANES), f32),
     ]
+    points = lat_rows * lon_cols
+    chunks = -(-points // DEPTH)
+    group = loads_group(lat_rows, lon_cols)
 
     gradient = pl.pallas_call(
         functools.partial(kernel, n_lat, n_lon, total),
@@ -345,17 +384,21 @@
         out_specs=pl.BlockSpec(memory_space=pltpu.VMEM),
         scratch_shapes=[
             pltpu.VMEM((lat_rows, lon_cols, modes), f32),
-            pltpu.VMEM((lat_rows, lon_cols, modes), bf16),
-            pltpu.VMEM((lat_rows, lon_cols, modes), bf16),
-            pltpu.VMEM((lat_rows, modes, lon_cols), bf16),
-            pltpu.VMEM((lat_rows, modes, lon_cols), bf16),
+            pltpu.VMEM((chunks * DEPTH, modes), f32),
+            pltpu.VMEM((chunks * DEPTH, 128), f32),
+            pltpu.VMEM((chunks, DEPTH, modes), bf16),
+            pltpu.VMEM((chunks, DEPTH, modes), bf16),
+            pltpu.VMEM((chunks, modes, DEPTH), bf16),
+            pltpu.VMEM((chunks, modes, DEPTH), bf16),
+            pltpu.VMEM((chunks, DEPTH, modes), bf16),
+            pltpu.VMEM((chunks, DEPTH, modes), bf16),
             pltpu.VMEM((modes, modes), f32),
             pltpu.VMEM((modes, modes), f32),
             *bufs,
             *bufs,
-            pltpu.SemaphoreType.DMA((5, 2)),
-            pltpu.SemaphoreType.DMA((5, 2)),
-            pltpu.SemaphoreType.DMA((lat_rows,)),
+            pltpu.SemaphoreType.DMA((6, 2)),
+            pltpu.SemaphoreType.DMA((6, 2)),
+            pltpu.SemaphoreType.DMA((lat_rows // group,)),
         ],
         compiler_params=pltpu.CompilerParams(
             collective_id=0, has_side_effects=True, vmem_limit_bytes=60 * 1024 * 1024

time: 73.7 us -> 63.5 us (0.86)
  Pallas kernels: 72.9 us -> 62.7 us
    pallas_call x1, Pallas kernels: 56.8 us -> 49.7 us  [shards(): pl.pallas_call(functools.partial(kernel, n_lat, n_lon, total), out_shape=...]
    pallas_call x1, Pallas kernels: 16.1 us -> 13 us  [shards(): pl.pallas_call(turn, out_shape=(jax.ShapeDtypeStruct(loadings.shape, f32)...]
where the time goes in v2:
time: 63.5 us; the launch traced here: 63.4 us
  Pallas kernels  62.7 us (99%)
  between operations  0.64 us (1%)
    pallas_call x1, Pallas kernels, shards(): pl.pallas_call(functools.partial(kernel, n_lat, n_lon, total), out_shape=...  49.7 us
    pallas_call x1, Pallas kernels, shards(): pl.pallas_call(turn, out_shape=(jax.ShapeDtypeStruct(loadings.shape, f32)...  13 us

profile of v2, /device:TPU:0, one launch (start us, length us, event | category | flops | bytes accessed | tf_op | source)
XLA Modules:
  0.0 63.4 jit_solution(10295005420090660892)
XLA Ops:
  0.6 49.7 %shard_map.41.gradient = f32[200,200]{1,0:T(8,128)} custom-call(f32[3,176]{1,0:T(4,128)} %constant.2.clone.weights, f32[22,180,200]{2,1,0:T(8,128)} %loadings.3), custom_call_target="tpu_custom_call" | custom-call | tf_op jit(solution)/shard_map/pallas_call | solution.py:377
  50.4 13.0 %shard_map.42 = (f32[22,180,200]{2,1,0:T(8,128)}, f32[200,200]{1,0:T(8,128)}) custom-call(f32[200,200]{1,0:T(8,128)} %shard_map.41.gradient, f32[22,180,200]{2,1,0:T(8,128)} %loadings.3), custom_call_target="tpu_custom_call" | custom-call | tf_op jit(solution)/shard_map/pallas_call | solution.py:407
